TPU v7x, 32 devices: a whole 2x2x4 slice. The times are simulated.
32 devices in a mesh: samp: 16 (over z, y, x), feat: 2 (over core).
Axes of the slice: x: 2, y: 2, z: 4, core: 2. Of those that a mesh axis runs over, the one named last changes fastest.
Arguments:
- design_matrix: bfloat16 [2048, 32768], P('samp', 'feat'), may hold values from -0.046875 to 0.046875
- labels: int32 [2048], P('samp'), may hold values from 0 to 1
- weights: float32 [16, 32768], P(None, ('feat', 'samp')), may hold values from -6 to 6
- lambdas: float32 [16], replicated, may hold values from 0.05 to 1
- sketch: bfloat16 [32768, 384], P(('feat', 'samp')), may hold values from -0.03125 to 0.03125
- sketch_values: float32 [384], replicated, may hold values from 0.05 to 2
Outputs:
- new_weights: float32 [16, 32768], P(None, ('feat', 'samp'))
All inputs are finite; a program needn't handle non-finite values.
Results may differ from a plain program's by a relative error of at most 0.004.
Values may be sent and summed in bfloat16 or wider, within the bound.
No kernel may reach another device: no remote copies, remote signals or barrier semaphores. Data moves between devices by JAX's collectives and lax.ppermute only.
A program may use at most 64 MiB of HBM per device.

v0:
```python
import jax
import jax.numpy as jnp
from jax import lax
from jax.sharding import PartitionSpec as P

ITERS = 2


def shards(design_matrix, labels, weights, lambdas, sketch, sketch_values):
    sketch_full = sketch.astype(jnp.float32)
    smallest = jnp.min(sketch_values)
    ratios = (smallest + lambdas[:, None]) / (sketch_values[None, :] + lambdas[:, None]) - 1.0

    def apply_rows(vector):
        vector_half = vector.astype(jnp.bfloat16)
        partial_rows = lax.dot_general(
            lax.all_gather(vector_half, "samp", axis=1, tiled=True),
            design_matrix,
            (((1,), (1,)), ((), ())),
            preferred_element_type=jnp.float32,
        )
        return lax.psum(partial_rows, "feat")

    def apply_columns(values):
        return lax.psum_scatter(
            lax.dot_general(
                design_matrix, values, (((0,), (1,)), ((), ())), preferred_element_type=jnp.float32
            ),
            "samp",
            scatter_dimension=0,
            tiled=True,
        ).T

    def precondition(residual):
        projected = jnp.dot(residual, sketch_full, precision=lax.Precision.HIGHEST)
        projected = lax.psum(projected, ("samp", "feat"))
        correction = lax.dot_general(
            ratios * projected,
            sketch_full,
            (((1,), (1,)), ((), ())),
            precision=lax.Precision.HIGHEST,
        )
        precond_res = residual + correction
        res_dot = lax.psum(jnp.sum(residual * precond_res, axis=1), ("samp", "feat"))
        return (precond_res, res_dot)

    logits = apply_rows(weights)
    probability = jax.nn.sigmoid(logits)
    hessian_diag = probability * (1.0 - probability)
    miss_rows = (probability - labels[None, :].astype(jnp.float32)).astype(jnp.bfloat16)
    gradient = apply_columns(miss_rows) + lambdas[:, None] * weights
    residual = -gradient
    precond_res, res_dot = precondition(residual)
    direction = precond_res
    update = jnp.zeros_like(residual)
    for iteration in range(ITERS):
        image_rows = apply_rows(direction)
        hess_dir = (
            apply_columns((hessian_diag * image_rows).astype(jnp.bfloat16))
            + lambdas[:, None] * direction
        )
        curvature = lax.psum(jnp.sum(direction * hess_dir, axis=1), ("samp", "feat"))
        step_size = res_dot / curvature
        update = update + step_size[:, None] * direction
        if iteration + 1 < ITERS:
            residual = residual - step_size[:, None] * hess_dir
            precond_res, new_dot = precondition(residual)
            direction = precond_res + (new_dot / res_dot)[:, None] * direction
            res_dot = new_dot
    return weights + update


def solution(mesh):
    return jax.shard_map(
        shards,
        mesh=mesh,
        in_specs=(
            P("samp", "feat"),
            P("samp"),
            P(None, ("feat", "samp")),
            P(),
            P(("feat", "samp"), None),
            P(),
        ),
        out_specs=P(None, ("feat", "samp")),
        check_vma=False,
    )
```

profile of v0, /device:TPU:10, one launch (start us, length us, event | category | flops | bytes accessed | tf_op | source)
XLA Modules:
  0.0 596.1 jit_solution(18189731865618623638)
XLA Ops:
  6.5 0.0 copy-start
  6.5 0.0 reduce-scatter.4.cloned.1.call-start
  6.5 0.7 convert_element_type.24
  7.3 0.8 convert_element_type.23
  8.1 33.0 %all_gather.9 = bf16[16,16384]{1,0:T(8,128)(2,1)S(1)} all-gather(bf16[16,1024]{1,0:T(8,128)(2,1)S(1)} %convert_element_type.23), channel_id=1, replica_groups=mesh['samp'=16,'feat'=2] {'samp'}, dimensions={1}, use_global_device_ids=true | all-gather | bytes 557056 | tf_op jit(solution)/shard_map/all_gather | solution.py:17
  41.1 3.4 fusion.22
  44.4 0.0 copy-start.3
  44.4 0.0 copy-start.2
  44.4 0.0 copy-start.1
  44.5 2.6 psum.63
  47.1 3.8 convolution_bitcast_fusion.2
  51.0 0.0 reduce-scatter.4.cloned.1.call-update
  51.0 0.0 reduce-scatter.6.cloned.1.call-start
  51.0 0.0 copy-done.3
  51.0 0.6 reduce_min.9
  51.6 0.0 copy-done.2
  51.6 0.6 broadcast_add_fusion
  52.3 73.3 %reduce-scatter.4.cloned.1.call-done = f32[1024,16]{0,1:T(8,128)} async-done(((f32[16384,16]{0,1:T(8,128)}), f32[1024,16]{0,1:T(8,128)}) %reduce-scatter.4.cloned.1.call-update) | async-done | bytes 65552 | tf_op jit(solution)/shard_map/reduce_scatter | solution.py:25
  125.6 0.0 copy-done.1
  125.6 0.9 fusion.2
  126.6 0.0 copy-done
  126.6 0.4 fusion.23
  127.0 50.1 %psum.64 = f32[16,384]{1,0:T(8,128)S(1)} all-reduce(f32[16,384]{1,0:T(8,128)S(1)} %fusion.23), channel_id=1, replica_groups=mesh['samp'=16,'feat'=2] {'samp','feat'}, use_global_device_ids=true, to_apply=%region_3.0 | all-reduce | flops 6144 | bytes 49152 | tf_op jit(solution)/shard_map/psum | solution.py:36
  177.1 0.7 fusion.21
  177.8 32.0 %all_gather.10 = bf16[16,16384]{1,0:T(8,128)(2,1)S(1)} all-gather(bf16[16,1024]{1,0:T(8,128)(2,1)S(1)} %get-tuple-element.9), channel_id=1, replica_groups=mesh['samp'=16,'feat'=2] {'samp'}, dimensions={1}, use_global_device_ids=true | all-gather | bytes 557056 | tf_op jit(solution)/shard_map/all_gather | solution.py:17
  209.8 3.4 fusion.24
  213.1 2.5 psum.66
  215.6 3.8 convolution_bitcast_fusion.1
  219.5 0.0 reduce-scatter.6.cloned.1.call-update
  219.5 0.0 reduce-scatter.8.cloned.1.call-start
  219.5 71.6 %reduce-scatter.6.cloned.1.call-done = f32[1024,16]{0,1:T(8,128)} async-done(((f32[16384,16]{0,1:T(8,128)}), f32[1024,16]{0,1:T(8,128)}) %reduce-scatter.6.cloned.1.call-update) | async-done | bytes 65552 | tf_op jit(solution)/shard_map/reduce_scatter | solution.py:25
  291.1 1.0 multiply_reduce_fusion.1
  292.1 49.7 %all-reduce = (f32[16]{0:T(128)S(1)}, f32[16]{0:T(128)S(1)}) all-reduce(f32[16]{0:T(128)S(1)} %get-tuple-element.6, f32[16]{0:T(128)S(1)} %get-tuple-element.5), channel_id=1, replica_groups=mesh['samp'=16,'feat'=2] {'samp','feat'}, use_global_device_ids=true, to_apply=%region_5.0 | all-reduce | flops 32 | bytes 256 | tf_op jit(solution)/shard_map/psum | solution.py:44
  341.9 0.9 multiply_subtract_fusion
  342.8 0.4 fusion.25
  343.2 38.3 %psum.68 = f32[16,384]{1,0:T(8,128)S(1)} all-reduce(f32[16,384]{1,0:T(8,128)S(1)} %fusion.25), channel_id=1, replica_groups=mesh['samp'=16,'feat'=2] {'samp','feat'}, use_global_device_ids=true, to_apply=%region_10.0 | all-reduce | flops 6144 | bytes 49152 | tf_op jit(solution)/shard_map/psum | solution.py:36
  381.5 0.8 multiply_reduce_fusion
  382.3 41.9 %psum.69 = f32[16]{0:T(128)S(1)} all-reduce(f32[16]{0:T(128)S(1)} %get-tuple-element.11), channel_id=1, replica_groups=mesh['samp'=16,'feat'=2] {'samp','feat'}, use_global_device_ids=true, to_apply=%region_12.0 | all-reduce | flops 16 | bytes 128 | tf_op jit(solution)/shard_map/psum | solution.py:44
  424.2 0.1 fusion.20
  424.3 31.8 %all_gather.11 = bf16[16,16384]{1,0:T(8,128)(2,1)S(1)} all-gather(bf16[16,1024]{1,0:T(8,128)(2,1)S(1)} %fusion.20), channel_id=1, replica_groups=mesh['samp'=16,'feat'=2] {'samp'}, dimensions={1}, use_global_device_ids=true | all-gather | bytes 557056 | tf_op jit(solution)/shard_map/all_gather | solution.py:17
  456.1 3.4 fusion.26
  459.5 2.5 psum.70
  462.0 3.9 convolution_bitcast_fusion
  465.8 0.0 reduce-scatter.8.cloned.1.call-update
  465.8 72.2 %reduce-scatter.8.cloned.1.call-done = f32[1024,16]{0,1:T(8,128)} async-done(((f32[16384,16]{0,1:T(8,128)}), f32[1024,16]{0,1:T(8,128)}) %reduce-scatter.8.cloned.1.call-update) | async-done | bytes 65552 | tf_op jit(solution)/shard_map/reduce_scatter | solution.py:25
  538.1 1.0 fusion.1
  539.1 49.8 %psum.71 = f32[16]{0:T(128)S(1)} all-reduce(f32[16]{0:T(128)S(1)} %fusion.1), channel_id=1, replica_groups=mesh['samp'=16,'feat'=2] {'samp','feat'}, use_global_device_ids=true, to_apply=%region_16.0 | all-reduce | flops 16 | bytes 128 | tf_op jit(solution)/shard_map/psum | solution.py:62
  588.9 0.7 add_add_fusion
  (3 shorter events, 0.0 us)
Async XLA Ops:
  6.5 120.0 %copy-start = (bf16[1024,384]{1,0:T(8,128)(2,1)S(1)}, bf16[1024,384]{1,0:T(8,128)(2,1)}, u32[]{:S(2)}) copy-start(bf16[1024,384]{1,0:T(8,128)(2,1)} %param.10) | copy-start | bytes 2359300
  6.5 119.1 %reduce-scatter.4.cloned.1.call-start = ((), (), s32[]{:S(2)}) async-start(), calls=%async_computation.3 | async-start | bytes 1114112 | tf_op jit(solution)/shard_map/reduce_scatter | solution.py:25
  44.4 6.6 %copy-start.3 = (f32[384]{0:T(512)S(1)}, f32[384]{0:T(512)}, u32[]{:S(2)}) copy-start(f32[384]{0:T(512)} %param.11) | copy-start | bytes 4612
  44.4 7.2 %copy-start.2 = (f32[16]{0:T(128)S(1)}, f32[16]{0:T(128)}, u32[]{:S(2)}) copy-start(f32[16]{0:T(128)} %param.9) | copy-start | bytes 196
  44.4 81.2 %copy-start.1 = (f32[16,1024]{1,0:T(8,128)S(1)}, f32[16,1024]{1,0:T(8,128)}, u32[]{:S(2)}) copy-start(f32[16,1024]{1,0:T(8,128)} %param.8) | copy-start | bytes 196612
  51.0 240.1 %reduce-scatter.6.cloned.1.call-start = ((), (), s32[]{:S(2)}) async-start(), calls=%async_computation.4 | async-start | bytes 1114112 | tf_op jit(solution)/shard_map/reduce_scatter | solution.py:25
  219.5 318.6 %reduce-scatter.8.cloned.1.call-start = ((), (), s32[]{:S(2)}) async-start(), calls=%async_computation.5 | async-start | bytes 1114112 | tf_op jit(solution)/shard_map/reduce_scatter | solution.py:25
Sparse Core Ops, SparseCore 0:
  51.1 74.4 reduce-scatter.3
  219.6 71.4 reduce-scatter.5
  466.0 72.0 reduce-scatter.7
where the time goes:
time: 597 us; the launch traced here: 596 us
  blocking collectives  334 us (56%)
  waiting for transfers between devices  217 us (36%)
  matrix products  24.1 us (4%)
  between operations  13.2 us (2%)
  other arithmetic  7.54 us (1%)
    reduce_scatter x3, waiting for transfers between devices, apply_columns(): lax.psum_scatter(lax.dot_general(design_matrix, values, (((0,), (1,)), ((...  217 us
    all_gather x3, blocking collectives, apply_rows(): lax.all_gather(vector_half, 'samp', axis=1, tiled=True)  96.7 us
    psum x2, blocking collectives, precondition(): lax.psum(jnp.sum(residual * precond_res, axis=1), ('samp', 'feat'))  91.6 us
    psum x2, blocking collectives, precondition(): projected = lax.psum(projected, ('samp', 'feat'))  88.3 us
    psum x1, blocking collectives, shards(): lax.psum(jnp.sum(direction * hess_dir, axis=1), ('samp', 'feat'))  49.8 us
  transfers between devices with their start and end apart: 3, of which 3 were waited for; matrix products, arithmetic and copies ran while one was open for 0% of the time, Pallas kernels for 0%

commit v1 on v0

--- a/solution.py
+++ b/solution.py
@@ -59,7 +59,8 @@
             apply_columns((hessian_diag * image_rows).astype(jnp.bfloat16))
             + lambdas[:, None] * direction
         )
-        curvature = lax.psum(jnp.sum(direction * hess_dir, axis=1), ("samp", "feat"))
+        watch_blocks = lambda incoming_x: lax.psum(lax.psum(incoming_x, "feat"), "samp")
+        curvature = watch_blocks(jnp.sum(direction * hess_dir, axis=1))
         step_size = res_dot / curvature
         update = update + step_size[:, None] * direction
         if iteration + 1 < ITERS:

time: 597 us -> 640 us (1.072); the launches traced: 596 us -> 631 us
  blocking collectives: 334 us -> 368 us
    psum x1 -> x4, blocking collectives: 49.8 us -> 88.1 us  [the longest x2 83.2 us: shards(): lax.psum(lax.psum(incoming_x, 'feat'), 'samp')]
where the time goes in v1:
time: 640 us; the launch traced here: 631 us
  blocking collectives  368 us (58%)
  waiting for transfers between devices  218 us (34%)
  matrix products  24.1 us (4%)
  between operations  13.2 us (2%)
  other arithmetic  7.54 us (1%)
    reduce_scatter x3, waiting for transfers between devices, apply_columns(): lax.psum_scatter(lax.dot_general(design_matrix, values, (((0,), (1,)), ((...  218 us
    all_gather x3, blocking collectives, apply_rows(): lax.all_gather(vector_half, 'samp', axis=1, tiled=True)  96.5 us
    psum x2, blocking collectives, precondition(): projected = lax.psum(projected, ('samp', 'feat'))  89.5 us
    psum x2, blocking collectives, precondition(): lax.psum(jnp.sum(residual * precond_res, axis=1), ('samp', 'feat'))  86.1 us
    psum x2, blocking collectives, shards(): lax.psum(lax.psum(incoming_x, 'feat'), 'samp')  83.2 us
  transfers between devices with their start and end apart: 3, of which 3 were waited for; matrix products, arithmetic and copies ran while one was open for 0% of the time, Pallas kernels for 0%

profile of v1, /device:TPU:10, one launch (start us, length us, event | category | flops | bytes accessed | tf_op | source)
XLA Modules:
  0.0 631.0 jit_solution(8417049769428493381)
XLA Ops:
  6.5 0.0 copy-start
  6.5 0.0 reduce-scatter.4.cloned.1.call-start
  6.5 0.7 convert_element_type.24
  7.3 0.8 convert_element_type.23
  8.1 33.0 %all_gather.9 = bf16[16,16384]{1,0:T(8,128)(2,1)S(1)} all-gather(bf16[16,1024]{1,0:T(8,128)(2,1)S(1)} %convert_element_type.23), channel_id=1, replica_groups=mesh['samp'=16,'feat'=2] {'samp'}, dimensions={1}, use_global_device_ids=true | all-gather | bytes 557056 | tf_op jit(solution)/shard_map/all_gather | solution.py:17
  41.1 3.4 fusion.22
  44.4 0.0 copy-start.1
  44.5 2.6 psum.77
  47.1 3.8 convolution_bitcast_fusion.2
  51.0 0.0 reduce-scatter.4.cloned.1.call-update
  51.0 0.0 reduce-scatter.6.cloned.1.call-start
  51.0 0.0 copy-done.3
  51.0 0.6 reduce_min.9
  51.6 0.0 copy-done.2
  51.6 0.6 broadcast_add_fusion
  52.3 73.3 %reduce-scatter.4.cloned.1.call-done = f32[1024,16]{0,1:T(8,128)} async-done(((f32[16384,16]{0,1:T(8,128)}), f32[1024,16]{0,1:T(8,128)}) %reduce-scatter.4.cloned.1.call-update) | async-done | bytes 65552 | tf_op jit(solution)/shard_map/reduce_scatter | solution.py:25
  125.6 0.0 copy-done.1
  125.6 0.9 fusion.2
  126.6 0.4 fusion.23
  127.0 50.1 %psum.78 = f32[16,384]{1,0:T(8,128)S(1)} all-reduce(f32[16,384]{1,0:T(8,128)S(1)} %fusion.23), channel_id=1, replica_groups=mesh['samp'=16,'feat'=2] {'samp','feat'}, use_global_device_ids=true, to_apply=%region_3.0 | all-reduce | flops 6144 | bytes 49152 | tf_op jit(solution)/shard_map/psum | solution.py:36
  177.1 0.7 fusion.21
  177.8 32.0 %all_gather.10 = bf16[16,16384]{1,0:T(8,128)(2,1)S(1)} all-gather(bf16[16,1024]{1,0:T(8,128)(2,1)S(1)} %get-tuple-element.7), channel_id=1, replica_groups=mesh['samp'=16,'feat'=2] {'samp'}, dimensions={1}, use_global_device_ids=true | all-gather | bytes 557056 | tf_op jit(solution)/shard_map/all_gather | solution.py:17
  209.8 3.4 fusion.24
  213.1 2.5 psum.80
  215.6 3.8 convolution_bitcast_fusion.1
  219.5 0.0 reduce-scatter.6.cloned.1.call-update
  219.5 0.0 reduce-scatter.8.cloned.1.call-start
  219.5 71.6 %reduce-scatter.6.cloned.1.call-done = f32[1024,16]{0,1:T(8,128)} async-done(((f32[16384,16]{0,1:T(8,128)}), f32[1024,16]{0,1:T(8,128)}) %reduce-scatter.6.cloned.1.call-update) | async-done | bytes 65552 | tf_op jit(solution)/shard_map/reduce_scatter | solution.py:25
  291.1 1.0 multiply_reduce_fusion.1
  292.1 2.5 psum.81
  294.6 41.5 %psum.82 = f32[16]{0:T(128)S(1)} all-reduce(f32[16]{0:T(128)S(1)} %psum.81), channel_id=1, replica_groups=mesh['samp'=16,'feat'=2] {'samp'}, use_global_device_ids=true, to_apply=%region_10.0 | all-reduce | flops 16 | bytes 128 | tf_op jit(solution)/shard_map/psum | solution.py:62
  336.0 45.4 %psum.79 = f32[16]{0:T(128)S(1)} all-reduce(f32[16]{0:T(128)S(1)} %get-tuple-element.6), channel_id=1, replica_groups=mesh['samp'=16,'feat'=2] {'samp','feat'}, use_global_device_ids=true, to_apply=%region_5.0 | all-reduce | flops 16 | bytes 128 | tf_op jit(solution)/shard_map/psum | solution.py:44
  381.5 0.9 multiply_subtract_fusion
  382.4 0.4 fusion.25
  382.8 39.4 %psum.83 = f32[16,384]{1,0:T(8,128)S(1)} all-reduce(f32[16,384]{1,0:T(8,128)S(1)} %fusion.25), channel_id=1, replica_groups=mesh['samp'=16,'feat'=2] {'samp','feat'}, use_global_device_ids=true, to_apply=%region_11.0 | all-reduce | flops 6144 | bytes 49152 | tf_op jit(solution)/shard_map/psum | solution.py:36
  422.3 0.8 multiply_reduce_fusion
  423.1 40.7 %psum.84 = f32[16]{0:T(128)S(1)} all-reduce(f32[16]{0:T(128)S(1)} %get-tuple-element.9), channel_id=1, replica_groups=mesh['samp'=16,'feat'=2] {'samp','feat'}, use_global_device_ids=true, to_apply=%region_13.0 | all-reduce | flops 16 | bytes 128 | tf_op jit(solution)/shard_map/psum | solution.py:44
  463.8 0.1 fusion.20
  463.9 31.5 %all_gather.11 = bf16[16,16384]{1,0:T(8,128)(2,1)S(1)} all-gather(bf16[16,1024]{1,0:T(8,128)(2,1)S(1)} %fusion.20), channel_id=1, replica_groups=mesh['samp'=16,'feat'=2] {'samp'}, dimensions={1}, use_global_device_ids=true | all-gather | bytes 557056 | tf_op jit(solution)/shard_map/all_gather | solution.py:17
  495.4 3.4 fusion.26
  498.8 2.5 psum.85
  501.3 3.9 convolution_bitcast_fusion
  505.1 0.0 reduce-scatter.8.cloned.1.call-update
  505.2 73.3 %reduce-scatter.8.cloned.1.call-done = f32[1024,16]{0,1:T(8,128)} async-done(((f32[16384,16]{0,1:T(8,128)}), f32[1024,16]{0,1:T(8,128)}) %reduce-scatter.8.cloned.1.call-update) | async-done | bytes 65552 | tf_op jit(solution)/shard_map/reduce_scatter | solution.py:25
  578.5 1.0 fusion.1
  579.5 2.5 psum.86
  582.0 41.7 %psum.87 = f32[16]{0:T(128)S(1)} all-reduce(f32[16]{0:T(128)S(1)} %psum.86), channel_id=1, replica_groups=mesh['samp'=16,'feat'=2] {'samp'}, use_global_device_ids=true, to_apply=%region_18.0 | all-reduce | flops 16 | bytes 128 | tf_op jit(solution)/shard_map/psum | solution.py:62
  623.7 0.7 add_add_fusion
  (6 shorter events, 0.0 us)
Async XLA Ops:
  6.5 120.0 %copy-start = (bf16[1024,384]{1,0:T(8,128)(2,1)S(1)}, bf16[1024,384]{1,0:T(8,128)(2,1)}, u32[]{:S(2)}) copy-start(bf16[1024,384]{1,0:T(8,128)(2,1)} %param.10) | copy-start | bytes 2359300
  6.5 119.1 %reduce-scatter.4.cloned.1.call-start = ((), (), s32[]{:S(2)}) async-start(), calls=%async_computation.3 | async-start | bytes 1114112 | tf_op jit(solution)/shard_map/reduce_scatter | solution.py:25
  44.4 6.6 %copy-start.3 = (f32[384]{0:T(512)S(1)}, f32[384]{0:T(512)}, u32[]{:S(2)}) copy-start(f32[384]{0:T(512)} %param.11) | copy-start | bytes 4612
  44.4 7.2 %copy-start.2 = (f32[16]{0:T(128)S(1)}, f32[16]{0:T(128)}, u32[]{:S(2)}) copy-start(f32[16]{0:T(128)} %param.9) | copy-start | bytes 196
  44.4 81.2 %copy-start.1 = (f32[16,1024]{1,0:T(8,128)S(1)}, f32[16,1024]{1,0:T(8,128)}, u32[]{:S(2)}) copy-start(f32[16,1024]{1,0:T(8,128)} %param.8) | copy-start | bytes 196612
  51.0 240.1 %reduce-scatter.6.cloned.1.call-start = ((), (), s32[]{:S(2)}) async-start(), calls=%async_computation.4 | async-start | bytes 1114112 | tf_op jit(solution)/shard_map/reduce_scatter | solution.py:25
  219.5 359.0 %reduce-scatter.8.cloned.1.call-start = ((), (), s32[]{:S(2)}) async-start(), calls=%async_computation.5 | async-start | bytes 1114112 | tf_op jit(solution)/shard_map/reduce_scatter | solution.py:25
Sparse Core Ops, SparseCore 0:
  51.1 74.4 reduce-scatter.3
  219.6 71.4 reduce-scatter.5
  505.3 73.1 reduce-scatter.7
